TPU v7x, 32 devices: a whole 2x2x4 slice. The times are simulated.
32 devices in a mesh: ka: 16 (over z, y, core), ga: 2 (over x).
Axes of the slice: x: 2, y: 2, z: 4, core: 2. Of those that a mesh axis runs over, the one named last changes fastest.
Arguments:
- coeffs: bfloat16 [16, 240, 2, 64, 128], P('ka', 'ga'), may hold values from -0.44921875 to 0.44921875
- neighbour: int32 [16, 3], P('ka'), may hold values from 0 to 15, as said below
- shift_id: int32 [16, 3], P('ka'), may hold values from 0 to 7
- block_map: int32 [8, 240], replicated, may hold values from 0 to 239, as said below
Outputs:
- intersection: float32 [16, 3, 2, 64, 64], P('ka', None, None, 'ga')
Inputs may be any that keep to these rules, and one draw needn't show every extreme that they name: `neighbour`: the k-points are numbered helically. The three columns of row k hold (k + 1) mod 16, (k + 4) mod 16 and (k + 8) mod 16, in an order drawn for each row. `block_map`: each row is a permutation of the 240 blocks. Block j lies in G-slice j // 120. In every row, each G-slice receives exactly 20 of its blocks from one other G-slice, exactly 10 from each of the remaining other G-slices, and the rest from itself.
All inputs are finite; a program needn't handle non-finite values.
Results may differ from a plain program's by a relative error of at most 0.0003.
Values may be sent and summed in bfloat16 or wider, within the bound.
A program may use at most 128 MiB of HBM per device.

v0:
```python
import jax
import jax.numpy as jnp
from jax import lax
from jax.sharding import PartitionSpec as P


def shifted(block, axis, distance):
    devices = range(lax.axis_size(axis))
    route = [((i - distance) % len(devices), i) for i in devices]
    return lax.ppermute(block, axis, route)


def complex_intersection(bra_real, bra_imag, ket_real, ket_imag, form):
    real_part = jnp.einsum(form, bra_real, ket_real, preferred_element_type=jnp.float32)
    real_part = real_part + jnp.einsum(form, bra_imag, ket_imag, preferred_element_type=jnp.float32)
    imag_part = jnp.einsum(form, bra_real, ket_imag, preferred_element_type=jnp.float32)
    imag_part = imag_part - jnp.einsum(form, bra_imag, ket_real, preferred_element_type=jnp.float32)
    return jnp.stack([real_part, imag_part], axis=-3)


def slot_plan(
    home_slice, target_slice, sent_local, place_local, my_slice, slices, capacity, slab_blocks
):
    targets = jnp.arange(slices, dtype=jnp.int32)
    chosen = (home_slice == my_slice)[:, None, :] & (
        target_slice[:, None, :] == targets[None, :, None]
    )
    chosen = chosen & (targets != my_slice)[None, :, None]
    counted = jnp.cumsum(chosen.astype(jnp.int32), axis=2) - 1
    places = jnp.arange(capacity, dtype=jnp.int32)
    matched = (
        chosen[:, :, None, :] & (counted[:, :, None, :] == places[None, None, :, None])
    ).astype(jnp.int32)
    filled = jnp.sum(matched, axis=3)
    sent_block = jnp.sum(matched * sent_local[:, None, None, :], axis=3)
    where_to = jnp.sum(matched * place_local[:, None, None, :], axis=3) + (1 - filled) * slab_blocks
    pair_count = home_slice.shape[0]
    return (
        sent_block.reshape(pair_count, slices * capacity),
        where_to.reshape(pair_count, slices * capacity),
    )


def on_device(coeffs, neighbour, shift_id, block_map):
    k_local = coeffs.shape[0]
    slab_blocks = coeffs.shape[1]
    band_count = coeffs.shape[3]
    lane_width = coeffs.shape[4]
    vector_count = neighbour.shape[1]
    cycle_size = lax.axis_size("ka")
    slices = lax.axis_size("ga")
    my_cycle = lax.axis_index("ka")
    my_slice = lax.axis_index("ga")
    capacity = 2 * max(1, slab_blocks // 12)
    all_blocks = slab_blocks * slices
    pair_count = k_local * vector_count
    k_total = k_local * cycle_size
    row_points = min(16, k_total // 4)
    row_devices = row_points // k_local
    pad_spec = ((0, 0), (0, 1), (0, 0), (0, 0), (0, 0))
    row_point = shifted(coeffs, "ka", -1)
    row_source = jnp.mod(my_cycle + 1, cycle_size)
    plane_kets = shifted(coeffs, "ka", -row_devices)
    plane_source = jnp.mod(my_cycle + row_devices, cycle_size)
    opposite = shifted(coeffs, "ka", cycle_size // 2)
    targets_flat = neighbour.reshape(-1)
    shifts_flat = shift_id.reshape(-1)
    target_device = targets_flat // k_local
    target_lane = targets_flat - target_device * k_local
    ket_index = jnp.where(
        target_device == my_cycle,
        target_lane,
        jnp.where(
            target_device == row_source,
            k_local,
            jnp.where(
                target_device == plane_source,
                k_local + 1 + target_lane,
                2 * k_local + 1 + target_lane,
            ),
        ),
    )
    bra_index = jnp.arange(pair_count, dtype=jnp.int32) // vector_count
    picks = (
        shifts_flat[:, None] == jnp.arange(block_map.shape[0], dtype=jnp.int32)[None, :]
    ).astype(jnp.int32)
    relabel = jnp.sum(picks[:, :, None] * block_map[None, :, :], axis=1)
    dest_global = jnp.broadcast_to(jnp.arange(all_blocks, dtype=jnp.int32)[None, :], relabel.shape)
    source_slice = relabel // slab_blocks
    dest_slice = dest_global // slab_blocks
    source_local = relabel - source_slice * slab_blocks
    dest_local = dest_global - dest_slice * slab_blocks
    kets = jnp.pad(jnp.concatenate([coeffs, row_point, plane_kets, opposite], axis=0), pad_spec)
    own_source = lax.dynamic_slice_in_dim(relabel, my_slice * slab_blocks, slab_blocks, 1)
    self_place = jnp.where(
        own_source // slab_blocks == my_slice, own_source - my_slice * slab_blocks, slab_blocks
    )
    ket_self = kets[ket_index[:, None], self_place]
    ket_self = ket_self.reshape(k_local, vector_count, slab_blocks, 2, band_count, lane_width)
    local_terms = complex_intersection(
        coeffs[:, :, 0],
        coeffs[:, :, 1],
        ket_self[:, :, :, 0],
        ket_self[:, :, :, 1],
        "ksmw,kbsnw->kbmn",
    )
    sent_block, where_to = slot_plan(
        dest_slice, source_slice, dest_local, source_local, my_slice, slices, capacity, slab_blocks
    )
    payload = coeffs[bra_index[:, None], sent_block]
    owner = jnp.broadcast_to(ket_index[:, None], (pair_count, slices))
    blocks = lax.all_to_all(payload, "ga", split_axis=1, concat_axis=1, tiled=True)
    places_in = lax.all_to_all(where_to, "ga", split_axis=1, concat_axis=1, tiled=True)
    owners = lax.all_to_all(owner, "ga", split_axis=1, concat_axis=1, tiled=True)
    partner = kets[owners[:, 0][:, None], places_in]
    remote = complex_intersection(
        blocks[:, :, 0], blocks[:, :, 1], partner[:, :, 0], partner[:, :, 1], "ismw,isnw->imn"
    )
    summed_part = local_terms + remote.reshape(k_local, vector_count, 2, band_count, band_count)
    total = lax.psum(summed_part, "ga")
    row_count = band_count // slices
    return lax.dynamic_slice_in_dim(total, my_slice * row_count, row_count, 3)


def solution(mesh):
    in_specs = (P("ka", "ga", None, None, None), P("ka", None), P("ka", None), P())
    out_specs = P("ka", None, None, "ga", None)
    return jax.shard_map(
        on_device, mesh=mesh, in_specs=in_specs, out_specs=out_specs, check_vma=False
    )
```

profile of v0, /device:TPU:0, one launch (start us, length us, event | category | flops | bytes accessed | tf_op | source)
XLA Modules:
  0.0 407.5 jit_solution(8698845887954236146)
XLA Ops:
  6.5 5.5 %collective-permute-start = (bf16[1,120,2,64,128]{4,3,2,1,0:T(8,128)(2,1)}, bf16[1,120,2,64,128]{4,3,2,1,0:T(8,128)(2,1)}, u32[]{:S(2)}, u32[]{:S(2)}) collective-permute-start(bf16[1,120,2,64,128]{4,3,2,1,0:T(8,128)(2,1)} %param.4), channel_id=1, source_target_pairs={{2,0},{4,2},{6,4},{8,6},{10,8},{12,10},{14,12},{16,14},{18,16},{20... | collective-permute-start | bytes 11796488 | tf_op jit(solution)/shard_map/ppermute | solution.py:10
  12.0 0.4 collective-permute-start.1
  12.5 0.7 clamp_shift-left_fusion
  13.1 0.6 broadcast_in_dim.35
  13.7 3.2 all-to-all-start.1
  16.9 0.7 fusion.68
  17.6 0.8 multiply_reduce_fusion
  18.6 1.8 reduce-window.6
  20.5 0.1 copy.78
  20.6 0.1 copy.79
  20.8 3.1 select_reduce_fusion.1
  24.0 0.1 copy.83
  24.1 0.1 copy.84
  24.2 0.6 copy.85
  24.8 0.1 copy.80
  24.9 0.1 reshape.387
  25.0 3.3 all-to-all-start.2
  28.4 5.1 %gather_fusion.1 = bf16[120,2,64,128]{3,2,1,0:T(8,128)(2,1)} fusion(bf16[1,120,2,64,128]{4,3,2,1,0:T(8,128)(2,1)} %param.4, s32[120]{0:T(128)S(1)} %reshape.395), kind=kCustom, calls=%fused_computation.1 | custom fusion | bytes 7865280 | tf_op jit(solution)/shard_map/gather | solution.py:110
  33.5 5.4 %copy.81 = bf16[3,40,2,64,128]{4,3,0,2,1:T(8,128)(2,1)} copy(bf16[3,40,2,64,128]{4,3,2,1,0:T(8,128)(2,1)} %bitcast.179) | data formatting | bytes 7864320 | tf_op jit(solution)/shard_map/gather | solution.py:110
  38.9 5.5 %all-to-all-start = ((bf16[3,40,2,64,128]{4,3,0,2,1:T(8,128)(2,1)}), bf16[3,40,2,64,128]{4,3,0,2,1:T(8,128)(2,1)}, u32[]{:S(2)}, u32[]{:S(2)}) async-start(bf16[3,40,2,64,128]{4,3,0,2,1:T(8,128)(2,1)} %copy.81), calls=%async_computation | async-start | bytes 7864320 | tf_op jit(solution)/shard_map/all_to_all | solution.py:112
  44.4 0.2 all-reduce.4.cloned.1.call-start
  44.6 0.1 fusion.60
  44.7 0.1 reshape.389
  44.9 0.1 reshape.401
  45.0 43.7 %all-to-all-done = bf16[3,40,2,64,128]{4,3,0,2,1:T(8,128)(2,1)} async-done(((bf16[3,40,2,64,128]{4,3,0,2,1:T(8,128)(2,1)}), bf16[3,40,2,64,128]{4,3,0,2,1:T(8,128)(2,1)}, u32[]{:S(2)}, u32[]{:S(2)}) %all-to-all-start) | async-done | bytes 3932192 | tf_op jit(solution)/shard_map/all_to_all | solution.py:112
  88.7 4.5 %fusion.77 = (bf16[3,40,1,64,128]{4,3,0,2,1:T(8,128)(2,1)S(1)}, bf16[3,40,1,64,128]{4,3,0,2,1:T(8,128)(2,1)}) fusion(bf16[3,40,2,64,128]{4,3,0,2,1:T(8,128)(2,1)} %all-to-all-done), kind=kLoop, calls=%fused_computation.110 | loop fusion | bytes 7864320 | tf_op jit(solution)/shard_map/slice | solution.py:117
  93.2 4.5 %collective-permute-done = bf16[1,120,2,64,128]{4,3,2,1,0:T(8,128)(2,1)} collective-permute-done((bf16[1,120,2,64,128]{4,3,2,1,0:T(8,128)(2,1)}, bf16[1,120,2,64,128]{4,3,2,1,0:T(8,128)(2,1)}, u32[]{:S(2)}, u32[]{:S(2)}) %collective-permute-start) | collective-permute-done | bytes 3932192 | tf_op jit(solution)/shard_map/ppermute | solution.py:10
  97.7 83.4 %collective-permute-done.1 = bf16[1,120,2,64,128]{4,3,2,1,0:T(8,128)(2,1)} collective-permute-done((bf16[1,120,2,64,128]{4,3,2,1,0:T(8,128)(2,1)}, bf16[1,120,2,64,128]{4,3,2,1,0:T(8,128)(2,1)}, u32[]{:S(2)}, u32[]{:S(2)}) %collective-permute-start.1) | collective-permute-done | bytes 3932192 | tf_op jit(solution)/shard_map/ppermute | solution.py:10
  181.1 126.2 %collective-permute-done.2 = bf16[1,120,2,64,128]{4,3,2,1,0:T(8,128)(2,1)} collective-permute-done((bf16[1,120,2,64,128]{4,3,2,1,0:T(8,128)(2,1)}, bf16[1,120,2,64,128]{4,3,2,1,0:T(8,128)(2,1)}, u32[]{:S(2)}, u32[]{:S(2)}) %collective-permute-start.2) | collective-permute-done | bytes 3932192 | tf_op jit(solution)/shard_map/ppermute | solution.py:10
  307.4 12.7 %fusion.6 = bf16[4,121,2,64,128]{4,3,2,1,0:T(8,128)(2,1)} fusion(bf16[1,120,2,64,128]{4,3,2,1,0:T(8,128)(2,1)} %collective-permute-done.2, bf16[1,120,2,64,128]{4,3,2,1,0:T(8,128)(2,1)} %collective-permute-done.1, bf16[1,120,2,64,128]{4,3,2,1,0:T(8,128)(2,1)} %collective-permute-done, bf16[1,120,2,64,128]{4,3,2,1,0:T(8,128)(2,1)S(1)} %copy-done), kind=kLoop, calls=%fused_computation.10 | loop fusion | flops 103088128 | bytes 31588352 | tf_op jit(solution)/shard_map/concatenate | solution.py:93
  320.1 8.8 %gather_fusion.2 = bf16[120,2,64,128]{3,2,1,0:T(8,128)(2,1)} fusion(bf16[4,121,2,64,128]{4,3,2,1,0:T(8,128)(2,1)} %fusion.6, s32[120]{0:T(128)S(1)} %reshape.401), kind=kCustom, calls=%fused_computation.2 | custom fusion | bytes 7865280 | tf_op jit(solution)/shard_map/gather | solution.py:115
  328.9 3.1 copy.87
  332.1 0.6 fusion.23
  332.7 1.3 copy-done.2
  334.0 0.7 fusion.24
  334.7 25.5 %gather_fusion = bf16[360,2,64,128]{3,2,1,0:T(8,128)(2,1)} fusion(bf16[4,121,2,64,128]{4,3,2,1,0:T(8,128)(2,1)} %fusion.6, s32[360]{0:T(512)S(1)} %reshape.389), kind=kCustom, calls=%fused_computation | custom fusion | bytes 23595840 | tf_op jit(solution)/shard_map/gather | solution.py:98
  360.1 6.5 %copy.75 = bf16[360,2,64,128]{3,2,0,1:T(8,128)(2,1)S(1)} copy(bf16[360,2,64,128]{3,2,1,0:T(8,128)(2,1)} %gather_fusion) | data formatting | bytes 23592960 | tf_op jit(solution)/shard_map/gather | solution.py:98
  366.7 1.7 fusion.27
  368.4 1.7 fusion.36
  370.0 0.4 copy-done.3
  370.5 0.7 fusion.54
  371.2 0.7 fusion.52
  371.8 1.7 fusion.42
  373.5 1.7 fusion.48
  375.2 0.7 maximum_add_fusion
  375.9 22.9 %all-reduce.4.cloned.1.call-done = f32[1,3,2,64,64]{3,4,1,2,0:T(8,128)} async-done(((f32[1,3,2,64,64]{3,4,1,2,0:T(8,128)}), f32[1,3,2,64,64]{3,4,1,2,0:T(8,128)}) %all-reduce.4.cloned.1.call-update) | async-done | bytes 98320 | tf_op jit(solution)/shard_map/psum | solution.py:120
  398.8 1.0 constant_dynamic-slice_fusion
  399.9 0.8 copy.93
  (34 shorter events, 0.7 us)
Async XLA Ops:
  6.5 91.2 %collective-permute-start = (bf16[1,120,2,64,128]{4,3,2,1,0:T(8,128)(2,1)}, bf16[1,120,2,64,128]{4,3,2,1,0:T(8,128)(2,1)}, u32[]{:S(2)}, u32[]{:S(2)}) collective-permute-start(bf16[1,120,2,64,128]{4,3,2,1,0:T(8,128)(2,1)} %param.4), channel_id=1, source_target_pairs={{2,0},{4,2},{6,4},{8,6},{10,8},{12,10},{14,12},{16,14},{18,16},{20... | collective-permute-start | bytes 11796488 | tf_op jit(solution)/shard_map/ppermute | solution.py:10
  12.0 169.1 %collective-permute-start.1 = (bf16[1,120,2,64,128]{4,3,2,1,0:T(8,128)(2,1)}, bf16[1,120,2,64,128]{4,3,2,1,0:T(8,128)(2,1)}, u32[]{:S(2)}, u32[]{:S(2)}) collective-permute-start(bf16[1,120,2,64,128]{4,3,2,1,0:T(8,128)(2,1)} %param.4), channel_id=1, source_target_pairs={{8,0},{10,2},{12,4},{14,6},{16,8},{18,10},{20,12},{22,14},{24,16},... | collective-permute-start | bytes 11796488 | tf_op jit(solution)/shard_map/ppermute | solution.py:10
  12.5 294.9 %collective-permute-start.2 = (bf16[1,120,2,64,128]{4,3,2,1,0:T(8,128)(2,1)}, bf16[1,120,2,64,128]{4,3,2,1,0:T(8,128)(2,1)}, u32[]{:S(2)}, u32[]{:S(2)}) collective-permute-start(bf16[1,120,2,64,128]{4,3,2,1,0:T(8,128)(2,1)} %param.4), channel_id=1, source_target_pairs={{16,0},{18,2},{20,4},{22,6},{24,8},{26,10},{28,12},{30,14},{0,16},... | collective-permute-start | bytes 11796488 | tf_op jit(solution)/shard_map/ppermute | solution.py:10
  13.7 11.3 %all-to-all-start.1 = ((s32[3,2,1]{0,2,1:T(1,128)}), s32[3,2,1]{0,2,1:T(1,128)S(1)}, u32[]{:S(2)}, u32[]{:S(2)}) async-start(s32[3,2,1]{0,2,1:T(1,128)} %broadcast_in_dim.35), calls=%async_computation.1 | async-start | bytes 2048 | tf_op jit(solution)/shard_map/all_to_all | solution.py:114
  25.0 13.8 %all-to-all-start.2 = ((s32[3,2,20]{2,0,1:T(4,128)}), s32[3,2,20]{2,0,1:T(4,128)S(1)}, u32[]{:S(2)}, u32[]{:S(2)}) async-start(s32[3,2,20]{2,0,1:T(4,128)} %copy.85), calls=%async_computation.2 | async-start | bytes 8192 | tf_op jit(solution)/shard_map/all_to_all | solution.py:113
  38.9 49.9 %all-to-all-start = ((bf16[3,40,2,64,128]{4,3,0,2,1:T(8,128)(2,1)}), bf16[3,40,2,64,128]{4,3,0,2,1:T(8,128)(2,1)}, u32[]{:S(2)}, u32[]{:S(2)}) async-start(bf16[3,40,2,64,128]{4,3,0,2,1:T(8,128)(2,1)} %copy.81), calls=%async_computation | async-start | bytes 7864320 | tf_op jit(solution)/shard_map/all_to_all | solution.py:112
  44.4 354.5 %all-reduce.4.cloned.1.call-start = ((), (), s32[]{:S(2)}) async-start(), calls=%async_computation.3 | async-start | bytes 393216 | tf_op jit(solution)/shard_map/psum | solution.py:120
  88.7 218.6 %copy-start = (bf16[1,120,2,64,128]{4,3,2,1,0:T(8,128)(2,1)S(1)}, bf16[1,120,2,64,128]{4,3,2,1,0:T(8,128)(2,1)}, u32[]{:S(2)}) copy-start(bf16[1,120,2,64,128]{4,3,2,1,0:T(8,128)(2,1)} %param.4) | copy-start | bytes 11796484
  328.9 3.2 copy-start.4
  332.0 2.0 copy-start.2
  360.1 6.5 %copy-start.1 = (bf16[1,120,2,64,128]{4,3,2,1,0:T(8,128)(2,1)S(1)}, bf16[1,120,2,64,128]{4,3,2,1,0:T(8,128)(2,1)}, u32[]{:S(2)}) copy-start(bf16[1,120,2,64,128]{4,3,2,1,0:T(8,128)(2,1)} %param.4) | copy-start | bytes 11796484
  368.4 2.1 copy-start.3
Sparse Core Ops, SparseCore 0:
  376.0 22.7 all-reduce.3
where the time goes:
time: 408 us; the launch traced here: 407 us
  waiting for transfers between devices  281 us (69%)
  local copies, waits for them, and re-layouts  64.7 us (16%)
  other arithmetic  21 us (5%)
  starting transfers between devices  18.1 us (4%)
  between operations  13.6 us (3%)
  matrix products  9.31 us (2%)
    ppermute x3, waiting for transfers between devices, shifted(): return lax.ppermute(block, axis, route)  214 us
    all_to_all x1, waiting for transfers between devices, on_device(): lax.all_to_all(payload, 'ga', split_axis=1, concat_axis=1, tiled=True)  43.7 us
    gather x2, local copies, waits for them, and re-layouts, on_device(): ket_self = kets[ket_index[:, None], self_place]  32 us
    psum x1, waiting for transfers between devices, on_device(): total = lax.psum(summed_part, 'ga')  22.9 us
    concatenate x1, other arithmetic, on_device(): jnp.concatenate([coeffs, row_point, plane_kets, opposite], axis=0)  12.7 us
    gather x2, local copies, waits for them, and re-layouts, on_device(): partner = kets[owners[:, 0][:, None], places_in]  12 us
    gather x2, local copies, waits for them, and re-layouts, on_device(): payload = coeffs[bra_index[:, None], sent_block]  10.5 us
  transfers between devices with their start and end apart: 7, of which 5 were waited for; matrix products, arithmetic and copies ran while one was open for 6% of the time, Pallas kernels for 0%

commit v1 on v0

--- a/solution.py
+++ b/solution.py
@@ -117,7 +117,7 @@
         blocks[:, :, 0], blocks[:, :, 1], partner[:, :, 0], partner[:, :, 1], "ismw,isnw->imn"
     )
     summed_part = local_terms + remote.reshape(k_local, vector_count, 2, band_count, band_count)
-    total = lax.psum(summed_part, "ga")
+    total = jnp.sum(lax.all_gather(summed_part, "ga"), axis=0)
     row_count = band_count // slices
     return lax.dynamic_slice_in_dim(total, my_slice * row_count, row_count, 3)
 

time: 408 us -> 377 us (0.924)
  waiting for transfers between devices: 281 us -> 258 us
  between operations: 13.6 us -> 0.22 us
  blocking collectives: 0 us -> 6.34 us
    psum x1 -> x0, waiting for transfers between devices: 22.9 us -> none  [on_device(): total = lax.psum(summed_part, 'ga')]
    all_gather x0 -> x1, blocking collectives: none -> 6.34 us  [on_device(): total = jnp.sum(lax.all_gather(summed_part, 'ga'), axis=0)]
  transfers between devices with their start and end apart: 7 -> 6, of which waited for: 5 -> 4; matrix products, arithmetic and copies ran while one was open for 6% -> 7% of each run, Pallas kernels for 0% -> 0%
where the time goes in v1:
time: 377 us; the launch traced here: 376 us
  waiting for transfers between devices  258 us (68%)
  local copies, waits for them, and re-layouts  63.7 us (17%)
  other arithmetic  20.4 us (5%)
  starting transfers between devices  18.1 us (5%)
  matrix products  9.29 us (2%)
  blocking collectives  6.34 us (2%)
    ppermute x3, waiting for transfers between devices, shifted(): return lax.ppermute(block, axis, route)  214 us
    all_to_all x1, waiting for transfers between devices, on_device(): lax.all_to_all(payload, 'ga', split_axis=1, concat_axis=1, tiled=True)  43.9 us
    gather x2, local copies, waits for them, and re-layouts, on_device(): ket_self = kets[ket_index[:, None], self_place]  32 us
    concatenate x1, other arithmetic, on_device(): jnp.concatenate([coeffs, row_point, plane_kets, opposite], axis=0)  12.7 us
    gather x2, local copies, waits for them, and re-layouts, on_device(): partner = kets[owners[:, 0][:, None], places_in]  11.9 us
    gather x2, local copies, waits for them, and re-layouts, on_device(): payload = coeffs[bra_index[:, None], sent_block]  10.5 us
  transfers between devices with their start and end apart: 6, of which 4 were waited for; matrix products, arithmetic and copies ran while one was open for 7% of the time, Pallas kernels for 0%

profile of v1, /device:TPU:0, one launch (start us, length us, event | category | flops | bytes accessed | tf_op | source)
XLA Modules:
  0.0 375.8 jit_solution(2927511646687502225)
XLA Ops:
  0.0 5.5 %collective-permute-start = (bf16[1,120,2,64,128]{4,3,2,1,0:T(8,128)(2,1)}, bf16[1,120,2,64,128]{4,3,2,1,0:T(8,128)(2,1)}, u32[]{:S(2)}, u32[]{:S(2)}) collective-permute-start(bf16[1,120,2,64,128]{4,3,2,1,0:T(8,128)(2,1)} %param.4), channel_id=1, source_target_pairs={{2,0},{4,2},{6,4},{8,6},{10,8},{12,10},{14,12},{16,14},{18,16},{20... | collective-permute-start | bytes 11796488 | tf_op jit(solution)/shard_map/ppermute | solution.py:10
  5.5 0.4 collective-permute-start.1
  5.9 0.7 clamp_shift-left_fusion
  6.6 0.6 broadcast_in_dim.35
  7.2 3.2 all-to-all-start.1
  10.5 0.7 fusion.68
  11.2 0.8 multiply_reduce_fusion
  12.1 1.8 reduce-window.6
  14.0 0.1 copy.81
  14.2 0.1 copy.82
  14.4 3.1 select_reduce_fusion.1
  17.5 0.1 copy.86
  17.6 0.1 copy.87
  17.7 0.6 copy.88
  18.3 0.1 copy.83
  18.4 0.1 reshape.397
  18.6 3.3 all-to-all-start.2
  21.8 0.1 reshape.405
  21.9 5.1 %gather_fusion.1 = bf16[120,2,64,128]{3,2,1,0:T(8,128)(2,1)} fusion(bf16[1,120,2,64,128]{4,3,2,1,0:T(8,128)(2,1)} %param.4, s32[120]{0:T(128)S(1)} %reshape.405), kind=kCustom, calls=%fused_computation.1 | custom fusion | bytes 7865280 | tf_op jit(solution)/shard_map/gather | solution.py:110
  27.0 5.4 %copy.84 = bf16[3,40,2,64,128]{4,3,0,2,1:T(8,128)(2,1)} copy(bf16[3,40,2,64,128]{4,3,2,1,0:T(8,128)(2,1)} %bitcast.181) | data formatting | bytes 7864320 | tf_op jit(solution)/shard_map/gather | solution.py:110
  32.4 5.7 %all-to-all-start = ((bf16[3,40,2,64,128]{4,3,0,2,1:T(8,128)(2,1)}), bf16[3,40,2,64,128]{4,3,0,2,1:T(8,128)(2,1)}, u32[]{:S(2)}, u32[]{:S(2)}) async-start(bf16[3,40,2,64,128]{4,3,0,2,1:T(8,128)(2,1)} %copy.84), calls=%async_computation | async-start | bytes 7864320 | tf_op jit(solution)/shard_map/all_to_all | solution.py:112
  38.1 0.1 fusion.60
  38.2 0.1 reshape.399
  38.3 0.1 all_to_all.19
  38.4 0.1 reshape.411
  38.5 43.9 %all-to-all-done = bf16[3,40,2,64,128]{4,3,0,2,1:T(8,128)(2,1)} async-done(((bf16[3,40,2,64,128]{4,3,0,2,1:T(8,128)(2,1)}), bf16[3,40,2,64,128]{4,3,0,2,1:T(8,128)(2,1)}, u32[]{:S(2)}, u32[]{:S(2)}) %all-to-all-start) | async-done | bytes 3932192 | tf_op jit(solution)/shard_map/all_to_all | solution.py:112
  82.5 4.5 %fusion.77 = (bf16[3,40,1,64,128]{4,3,0,2,1:T(8,128)(2,1)S(1)}, bf16[3,40,1,64,128]{4,3,0,2,1:T(8,128)(2,1)}) fusion(bf16[3,40,2,64,128]{4,3,0,2,1:T(8,128)(2,1)} %all-to-all-done), kind=kLoop, calls=%fused_computation.110 | loop fusion | bytes 7864320 | tf_op jit(solution)/shard_map/slice | solution.py:117
  86.9 4.2 %collective-permute-done = bf16[1,120,2,64,128]{4,3,2,1,0:T(8,128)(2,1)} collective-permute-done((bf16[1,120,2,64,128]{4,3,2,1,0:T(8,128)(2,1)}, bf16[1,120,2,64,128]{4,3,2,1,0:T(8,128)(2,1)}, u32[]{:S(2)}, u32[]{:S(2)}) %collective-permute-start) | collective-permute-done | bytes 3932192 | tf_op jit(solution)/shard_map/ppermute | solution.py:10
  91.2 83.4 %collective-permute-done.1 = bf16[1,120,2,64,128]{4,3,2,1,0:T(8,128)(2,1)} collective-permute-done((bf16[1,120,2,64,128]{4,3,2,1,0:T(8,128)(2,1)}, bf16[1,120,2,64,128]{4,3,2,1,0:T(8,128)(2,1)}, u32[]{:S(2)}, u32[]{:S(2)}) %collective-permute-start.1) | collective-permute-done | bytes 3932192 | tf_op jit(solution)/shard_map/ppermute | solution.py:10
  174.6 126.2 %collective-permute-done.2 = bf16[1,120,2,64,128]{4,3,2,1,0:T(8,128)(2,1)} collective-permute-done((bf16[1,120,2,64,128]{4,3,2,1,0:T(8,128)(2,1)}, bf16[1,120,2,64,128]{4,3,2,1,0:T(8,128)(2,1)}, u32[]{:S(2)}, u32[]{:S(2)}) %collective-permute-start.2) | collective-permute-done | bytes 3932192 | tf_op jit(solution)/shard_map/ppermute | solution.py:10
  300.8 12.7 %fusion.6 = bf16[4,121,2,64,128]{4,3,2,1,0:T(8,128)(2,1)} fusion(bf16[1,120,2,64,128]{4,3,2,1,0:T(8,128)(2,1)} %collective-permute-done.2, bf16[1,120,2,64,128]{4,3,2,1,0:T(8,128)(2,1)} %collective-permute-done.1, bf16[1,120,2,64,128]{4,3,2,1,0:T(8,128)(2,1)} %collective-permute-done, bf16[1,120,2,64,128]{4,3,2,1,0:T(8,128)(2,1)S(1)} %copy-done), kind=kLoop, calls=%fused_computation.10 | loop fusion | flops 103088128 | bytes 31588352 | tf_op jit(solution)/shard_map/concatenate | solution.py:93
  313.6 8.8 %gather_fusion.2 = bf16[120,2,64,128]{3,2,1,0:T(8,128)(2,1)} fusion(bf16[4,121,2,64,128]{4,3,2,1,0:T(8,128)(2,1)} %fusion.6, s32[120]{0:T(128)S(1)} %reshape.411), kind=kCustom, calls=%fused_computation.2 | custom fusion | bytes 7865280 | tf_op jit(solution)/shard_map/gather | solution.py:115
  322.4 3.1 copy.90
  325.5 0.6 fusion.23
  326.2 1.3 copy-done.2
  327.5 0.6 fusion.24
  328.1 25.5 %gather_fusion = bf16[360,2,64,128]{3,2,1,0:T(8,128)(2,1)} fusion(bf16[4,121,2,64,128]{4,3,2,1,0:T(8,128)(2,1)} %fusion.6, s32[360]{0:T(512)S(1)} %reshape.399), kind=kCustom, calls=%fused_computation | custom fusion | bytes 23595840 | tf_op jit(solution)/shard_map/gather | solution.py:98
  353.6 6.5 %copy.78 = bf16[360,2,64,128]{3,2,0,1:T(8,128)(2,1)S(1)} copy(bf16[360,2,64,128]{3,2,1,0:T(8,128)(2,1)} %gather_fusion) | data formatting | bytes 23592960 | tf_op jit(solution)/shard_map/gather | solution.py:98
  360.1 1.7 fusion.27
  361.8 1.7 fusion.36
  363.5 0.4 copy-done.3
  363.9 0.7 fusion.54
  364.6 0.7 fusion.52
  365.3 1.7 fusion.42
  367.0 1.7 fusion.48
  368.7 0.1 copy.96
  368.8 6.3 %all_gather.4 = f32[2,1,3,2,64,64]{5,4,3,2,1,0:T(8,128)S(1)} all-gather(f32[1,1,3,2,64,64]{5,4,3,2,1,0:T(8,128)S(1)} %copy.96), channel_id=1, replica_groups=mesh['ka'=16,'ga'=2] {'ga'}, dimensions={0}, use_global_device_ids=true | all-gather | bytes 294912 | tf_op jit(solution)/shard_map/all_gather | solution.py:120
  375.2 0.7 dynamic-slice_bitcast_fusion
  (33 shorter events, 0.6 us)
Async XLA Ops:
  0.0 91.2 %collective-permute-start = (bf16[1,120,2,64,128]{4,3,2,1,0:T(8,128)(2,1)}, bf16[1,120,2,64,128]{4,3,2,1,0:T(8,128)(2,1)}, u32[]{:S(2)}, u32[]{:S(2)}) collective-permute-start(bf16[1,120,2,64,128]{4,3,2,1,0:T(8,128)(2,1)} %param.4), channel_id=1, source_target_pairs={{2,0},{4,2},{6,4},{8,6},{10,8},{12,10},{14,12},{16,14},{18,16},{20... | collective-permute-start | bytes 11796488 | tf_op jit(solution)/shard_map/ppermute | solution.py:10
  5.5 169.1 %collective-permute-start.1 = (bf16[1,120,2,64,128]{4,3,2,1,0:T(8,128)(2,1)}, bf16[1,120,2,64,128]{4,3,2,1,0:T(8,128)(2,1)}, u32[]{:S(2)}, u32[]{:S(2)}) collective-permute-start(bf16[1,120,2,64,128]{4,3,2,1,0:T(8,128)(2,1)} %param.4), channel_id=1, source_target_pairs={{8,0},{10,2},{12,4},{14,6},{16,8},{18,10},{20,12},{22,14},{24,16},... | collective-permute-start | bytes 11796488 | tf_op jit(solution)/shard_map/ppermute | solution.py:10
  5.9 294.9 %collective-permute-start.2 = (bf16[1,120,2,64,128]{4,3,2,1,0:T(8,128)(2,1)}, bf16[1,120,2,64,128]{4,3,2,1,0:T(8,128)(2,1)}, u32[]{:S(2)}, u32[]{:S(2)}) collective-permute-start(bf16[1,120,2,64,128]{4,3,2,1,0:T(8,128)(2,1)} %param.4), channel_id=1, source_target_pairs={{16,0},{18,2},{20,4},{22,6},{24,8},{26,10},{28,12},{30,14},{0,16},... | collective-permute-start | bytes 11796488 | tf_op jit(solution)/shard_map/ppermute | solution.py:10
  7.2 11.4 %all-to-all-start.1 = ((s32[3,2,1]{0,2,1:T(1,128)}), s32[3,2,1]{0,2,1:T(1,128)S(1)}, u32[]{:S(2)}, u32[]{:S(2)}) async-start(s32[3,2,1]{0,2,1:T(1,128)} %broadcast_in_dim.35), calls=%async_computation.1 | async-start | bytes 2048 | tf_op jit(solution)/shard_map/all_to_all | solution.py:114
  18.6 13.8 %all-to-all-start.2 = ((s32[3,2,20]{2,0,1:T(4,128)}), s32[3,2,20]{2,0,1:T(4,128)S(1)}, u32[]{:S(2)}, u32[]{:S(2)}) async-start(s32[3,2,20]{2,0,1:T(4,128)} %copy.88), calls=%async_computation.2 | async-start | bytes 8192 | tf_op jit(solution)/shard_map/all_to_all | solution.py:113
  32.4 50.0 %all-to-all-start = ((bf16[3,40,2,64,128]{4,3,0,2,1:T(8,128)(2,1)}), bf16[3,40,2,64,128]{4,3,0,2,1:T(8,128)(2,1)}, u32[]{:S(2)}, u32[]{:S(2)}) async-start(bf16[3,40,2,64,128]{4,3,0,2,1:T(8,128)(2,1)} %copy.84), calls=%async_computation | async-start | bytes 7864320 | tf_op jit(solution)/shard_map/all_to_all | solution.py:112
  82.5 218.4 %copy-start = (bf16[1,120,2,64,128]{4,3,2,1,0:T(8,128)(2,1)S(1)}, bf16[1,120,2,64,128]{4,3,2,1,0:T(8,128)(2,1)}, u32[]{:S(2)}) copy-start(bf16[1,120,2,64,128]{4,3,2,1,0:T(8,128)(2,1)} %param.4) | copy-start | bytes 11796484
  322.4 3.2 copy-start.4
  325.5 2.0 copy-start.2
  353.6 6.5 %copy-start.1 = (bf16[1,120,2,64,128]{4,3,2,1,0:T(8,128)(2,1)S(1)}, bf16[1,120,2,64,128]{4,3,2,1,0:T(8,128)(2,1)}, u32[]{:S(2)}) copy-start(bf16[1,120,2,64,128]{4,3,2,1,0:T(8,128)(2,1)} %param.4) | copy-start | bytes 11796484
  361.8 2.1 copy-start.3
